TPU v7x, 32 devices: a whole 2x2x4 slice. The times are simulated.
32 devices in a mesh: task: 2 (over x), dp: 8 (over z, core), mp: 2 (over y).
Axes of the slice: x: 2, y: 2, z: 4, core: 2. Of those that a mesh axis runs over, the one named last changes fastest.
Arguments:
- deltas: bfloat16 [6, 2048, 4608], P('task', 'dp', 'mp'), may hold values from -400 to 400, as said below
- fishers: bfloat16 [6, 2048, 4608], P('task', 'dp', 'mp'), may hold values from 0.0009994507 to 1
Outputs:
- merged_out: float32 [2048, 4608], P('dp', 'mp')
Inputs may be any that keep to these rules, and one draw needn't show every extreme that they name: `deltas`: Real-valued weight differences.
All inputs are finite; a program needn't handle non-finite values.
Results may differ from a plain program's by a relative error of at most 0.0003.
Values sent between devices are 32-bit elements; how exact they have to be, the bound alone decides.
A program may use at most 64 MiB of HBM per device.

v0:
```python
import jax
import jax.numpy as jnp
from jax import lax
from jax.sharding import PartitionSpec as P


def task_squares(deltas):
    widened = deltas.astype(jnp.float32)
    own_sums = jnp.sum(widened * widened, axis=(1, 2))
    held_tasks = deltas.shape[0]
    slot_sums = jnp.zeros((held_tasks * lax.axis_size("task"),), jnp.float32)
    return lax.dynamic_update_slice(slot_sums, own_sums, (lax.axis_index("task") * held_tasks,))


def shards(deltas, fishers):
    weights = fishers.astype(jnp.float32)
    numerator = jnp.sum(weights * deltas.astype(jnp.float32), axis=0)
    denominator = jnp.sum(weights, axis=0)
    task_part = task_squares(deltas)
    task_sq = lax.psum(task_part, ("task", "dp", "mp"))
    numerator, denominator = (
        lax.psum_scatter(numerator, "task", scatter_dimension=0, tiled=True),
        lax.psum_scatter(denominator, "task", scatter_dimension=0, tiled=True),
    )
    half_rows = numerator / denominator
    merged_part = jnp.sum(half_rows * half_rows)
    merged = lax.all_gather(half_rows, "task", axis=0, tiled=True)
    merged_sq = lax.psum(merged_part, ("task", "dp", "mp"))
    target = jnp.mean(jnp.sqrt(task_sq + 1e-06))
    rescale = target / jnp.sqrt(merged_sq + 1e-06)
    return rescale * merged


def solution(mesh):
    placed = (P("task", "dp", "mp"), P("task", "dp", "mp"))
    return jax.shard_map(
        shards, mesh=mesh, in_specs=placed, out_specs=P("dp", "mp"), check_vma=False
    )
```

profile of v0, /device:TPU:0, one launch (start us, length us, event | category | flops | bytes accessed | tf_op | source)
XLA Modules:
  0.0 144.6 jit_solution(8158411460100088740)
XLA Ops:
  6.5 0.0 reduce-scatter.3.cloned.1.call-start
  6.5 7.8 %fusion = (f32[3]{0:T(128)S(1)}, f32[256,2304]{1,0:T(8,128)}, f32[256,2304]{1,0:T(8,128)}) fusion(bf16[3,256,2304]{2,1,0:T(8,128)(2,1)} %param.2, bf16[3,256,2304]{2,1,0:T(8,128)(2,1)} %param.3), kind=kLoop, calls=%fused_computation.3 | loop fusion | flops 11206653 | bytes 11796492 | tf_op jit(solution)/shard_map/reduce_sum | solution.py:9
  14.4 0.0 reduce-scatter.3.cloned.1.call-update
  14.4 0.0 reduce-scatter.5.cloned.1.call-start
  14.4 0.7 reduce-scatter.5.cloned.1.call-update
  15.1 0.0 all-gather.2.cloned.1.call-start
  15.2 36.9 %reduce-scatter.3.cloned.1.call-done = f32[128,2304]{1,0:T(8,128)} async-done(((f32[256,2304]{1,0:T(8,128)}), f32[128,2304]{1,0:T(8,128)}) %reduce-scatter.3.cloned.1.call-update) | async-done | bytes 1179664 | tf_op jit(solution)/shard_map/reduce_scatter | solution.py:22
  52.1 37.0 %reduce-scatter.5.cloned.1.call-done = f32[128,2304]{1,0:T(8,128)} async-done(((f32[256,2304]{1,0:T(8,128)}), f32[128,2304]{1,0:T(8,128)}) %reduce-scatter.5.cloned.1.call-update) | async-done | bytes 1179664 | tf_op jit(solution)/shard_map/reduce_scatter | solution.py:23
  89.1 3.5 %multiply_reduce_fusion = (f32[]{:T(128)}, f32[128,2304]{1,0:T(8,128)}) fusion(f32[128,2304]{1,0:T(8,128)} %reduce-scatter.3.cloned.1.call-done, f32[128,2304]{1,0:T(8,128)} %reduce-scatter.5.cloned.1.call-done), kind=kLoop, calls=%fused_computation.6 | loop fusion | flops 884735 | bytes 3538948 | tf_op jit(solution)/shard_map/reduce_sum | solution.py:26
  92.6 0.0 all-gather.2.cloned.1.call-update
  92.6 0.2 dynamic_update_slice.3
  92.9 40.1 %all-reduce = (f32[6]{0:T(128)S(1)}, f32[]{:T(128)}) all-reduce(f32[6]{0:T(128)S(1)} %dynamic_update_slice.3, f32[]{:T(128)} %get-tuple-element.10), channel_id=1, replica_groups=mesh['task'=2,'dp'=8,'mp'=2] {'task','dp','mp'}, use_global_device_ids=true, to_apply=%region_1.0 | all-reduce | flops 7 | bytes 56 | tf_op jit(solution)/shard_map/psum | solution.py:20
  133.7 0.6 sqrt_reduce_fusion
  134.8 0.0 all-gather.2.cloned.1.call-done
  134.9 3.2 %broadcast_multiply_fusion = f32[256,2304]{1,0:T(8,128)} fusion(f32[256,2304]{1,0:T(8,128)} %all-gather.2.cloned.1.call-done, f32[]{:T(128)S(6)} %div.11), kind=kLoop, calls=%fused_computation.5 | loop fusion | flops 589824 | bytes 4718596 | tf_op jit(solution)/shard_map/mul | solution.py:31
  (1 shorter events, 0.0 us)
Async XLA Ops:
  6.5 45.5 %reduce-scatter.3.cloned.1.call-start = ((), (), s32[]{:S(2)}) async-start(), calls=%async_computation.2 | async-start | bytes 3538944 | tf_op jit(solution)/shard_map/reduce_scatter | solution.py:22
  14.4 74.7 %reduce-scatter.5.cloned.1.call-start = ((), (), s32[]{:S(2)}) async-start(), calls=%async_computation.3 | async-start | bytes 3538944 | tf_op jit(solution)/shard_map/reduce_scatter | solution.py:23
  15.1 119.7 %all-gather.2.cloned.1.call-start = ((), (), s32[]{:S(2)}) async-start(), calls=%async_computation.4 | async-start | bytes 3538944 | tf_op jit(solution)/shard_map/all_gather | solution.py:27
Sparse Core Ops, SparseCore 0:
  14.5 37.5 reduce-scatter.2
  54.3 34.7 reduce-scatter.4
  92.7 36.3 all-gather.1
where the time goes:
time: 145 us
  waiting for transfers between devices  74.7 us (52%)
  blocking collectives  40.1 us (28%)
  other arithmetic  15.1 us (10%)
  between operations  14.4 us (10%)
    psum x1, blocking collectives, shards(): task_sq = lax.psum(task_part, ('task', 'dp', 'mp'))  40.1 us
    reduce_scatter x1, waiting for transfers between devices, shards(): lax.psum_scatter(denominator, 'task', scatter_dimension=0, tiled=True)  37 us
    reduce_scatter x1, waiting for transfers between devices, shards(): lax.psum_scatter(numerator, 'task', scatter_dimension=0, tiled=True)  36.9 us
    reduce_sum x1, other arithmetic, task_squares(): own_sums = jnp.sum(widened * widened, axis=(1, 2))  7.82 us
    reduce_sum x1, other arithmetic, shards(): merged_part = jnp.sum(half_rows * half_rows)  3.47 us
    mul x1, other arithmetic, shards(): return rescale * merged  3.23 us
  transfers between devices with their start and end apart: 3, of which 2 were waited for; matrix products, arithmetic and copies ran while one was open for 1% of the time, Pallas kernels for 0%

commit v1 on v0

--- a/solution.py
+++ b/solution.py
@@ -17,7 +17,8 @@
     numerator = jnp.sum(weights * deltas.astype(jnp.float32), axis=0)
     denominator = jnp.sum(weights, axis=0)
     task_part = task_squares(deltas)
-    task_sq = lax.psum(task_part, ("task", "dp", "mp"))
+    pieces = lax.all_gather(task_part, ("task", "dp", "mp"))
+    task_sq = jnp.sum(pieces, axis=0)
     numerator, denominator = (
         lax.psum_scatter(numerator, "task", scatter_dimension=0, tiled=True),
         lax.psum_scatter(denominator, "task", scatter_dimension=0, tiled=True),

time: 145 us -> 209 us (1.44)
  blocking collectives: 40.1 us -> 104 us
    all_gather x0 -> x1, blocking collectives: none -> 67 us  [shards(): pieces = lax.all_gather(task_part, ('task', 'dp', 'mp'))]
    psum x1, blocking collectives: 40.1 us -> 37 us  [shards(): merged_sq = lax.psum(merged_part, ('task', 'dp', 'mp'))]
  transfers between devices with their start and end apart: 3 -> 3, of which waited for: 2 -> 2; matrix products, arithmetic and copies ran while one was open for 1% -> 0% of each run, Pallas kernels for 0% -> 0%
where the time goes in v1:
time: 209 us; the launch traced here: 208 us
  blocking collectives  104 us (50%)
  waiting for transfers between devices  74.7 us (36%)
  other arithmetic  15.2 us (7%)
  between operations  14.3 us (7%)
    all_gather x1, blocking collectives, shards(): pieces = lax.all_gather(task_part, ('task', 'dp', 'mp'))  67 us
    reduce_scatter x1, waiting for transfers between devices, shards(): lax.psum_scatter(denominator, 'task', scatter_dimension=0, tiled=True)  37 us
    psum x1, blocking collectives, shards(): merged_sq = lax.psum(merged_part, ('task', 'dp', 'mp'))  37 us
    reduce_scatter x1, waiting for transfers between devices, shards(): lax.psum_scatter(numerator, 'task', scatter_dimension=0, tiled=True)  36.9 us
    reduce_sum x1, other arithmetic, task_squares(): own_sums = jnp.sum(widened * widened, axis=(1, 2))  7.85 us
  transfers between devices with their start and end apart: 3, of which 2 were waited for; matrix products, arithmetic and copies ran while one was open for 0% of the time, Pallas kernels for 0%

profile of v1, /device:TPU:0, one launch (start us, length us, event | category | flops | bytes accessed | tf_op | source)
XLA Modules:
  0.0 208.4 jit_solution(5973919558160702079)
XLA Ops:
  6.5 0.0 reduce-scatter.3.cloned.1.call-start
  6.5 7.8 %fusion = (f32[3]{0:T(128)S(1)}, f32[256,2304]{1,0:T(8,128)}, f32[256,2304]{1,0:T(8,128)}) fusion(bf16[3,256,2304]{2,1,0:T(8,128)(2,1)} %param.2, bf16[3,256,2304]{2,1,0:T(8,128)(2,1)} %param.3), kind=kLoop, calls=%fused_computation.3 | loop fusion | flops 11206653 | bytes 11796492 | tf_op jit(solution)/shard_map/reduce_sum | solution.py:9
  14.4 0.0 reduce-scatter.3.cloned.1.call-update
  14.4 0.0 reduce-scatter.5.cloned.1.call-start
  14.5 0.7 reduce-scatter.5.cloned.1.call-update
  15.2 0.0 all-gather.3.cloned.1.call-start
  15.2 36.9 %reduce-scatter.3.cloned.1.call-done = f32[128,2304]{1,0:T(8,128)} async-done(((f32[256,2304]{1,0:T(8,128)}), f32[128,2304]{1,0:T(8,128)}) %reduce-scatter.3.cloned.1.call-update) | async-done | bytes 1179664 | tf_op jit(solution)/shard_map/reduce_scatter | solution.py:23
  52.1 37.0 %reduce-scatter.5.cloned.1.call-done = f32[128,2304]{1,0:T(8,128)} async-done(((f32[256,2304]{1,0:T(8,128)}), f32[128,2304]{1,0:T(8,128)}) %reduce-scatter.5.cloned.1.call-update) | async-done | bytes 1179664 | tf_op jit(solution)/shard_map/reduce_scatter | solution.py:24
  89.1 3.4 %multiply_reduce_fusion = (f32[]{:T(128)}, f32[128,2304]{1,0:T(8,128)}) fusion(f32[128,2304]{1,0:T(8,128)} %reduce-scatter.3.cloned.1.call-done, f32[128,2304]{1,0:T(8,128)} %reduce-scatter.5.cloned.1.call-done), kind=kLoop, calls=%fused_computation.6 | loop fusion | flops 884735 | bytes 3538948 | tf_op jit(solution)/shard_map/reduce_sum | solution.py:27
  92.6 0.0 all-gather.3.cloned.1.call-update
  92.6 0.1 dynamic_update_slice.5
  92.8 67.0 %all-gather = f32[32,1,6]{2,1,0:T(1,128)S(1)} all-gather(f32[1,1,6]{2,1,0:T(1,128)S(1)} %dynamic_update_slice.5), channel_id=1, replica_groups=mesh['task'=2,'dp'=8,'mp'=2] {'task','dp','mp'}, dimensions={0}, use_global_device_ids=true | all-gather | bytes 792 | tf_op jit(solution)/shard_map/all_gather | solution.py:20
  159.8 0.1 reduce_sum.55
  159.8 0.6 sqrt_reduce_fusion
  161.0 37.0 %psum.7 = f32[]{:T(128)} all-reduce(f32[]{:T(128)} %get-tuple-element.8), channel_id=1, replica_groups=mesh['task'=2,'dp'=8,'mp'=2] {'task','dp','mp'}, use_global_device_ids=true, to_apply=%region_8.0 | all-reduce | flops 1 | bytes 8 | tf_op jit(solution)/shard_map/psum | solution.py:29
  198.6 0.0 all-gather.3.cloned.1.call-done
  198.7 3.2 %broadcast_multiply_fusion = f32[256,2304]{1,0:T(8,128)} fusion(f32[256,2304]{1,0:T(8,128)} %all-gather.3.cloned.1.call-done, f32[]{:T(128)S(6)} %div.11), kind=kLoop, calls=%fused_computation.5 | loop fusion | flops 589824 | bytes 4718596 | tf_op jit(solution)/shard_map/mul | solution.py:32
  (1 shorter events, 0.0 us)
Async XLA Ops:
  6.5 45.6 %reduce-scatter.3.cloned.1.call-start = ((), (), s32[]{:S(2)}) async-start(), calls=%async_computation.2 | async-start | bytes 3538944 | tf_op jit(solution)/shard_map/reduce_scatter | solution.py:23
  14.4 74.7 %reduce-scatter.5.cloned.1.call-start = ((), (), s32[]{:S(2)}) async-start(), calls=%async_computation.3 | async-start | bytes 3538944 | tf_op jit(solution)/shard_map/reduce_scatter | solution.py:24
  15.2 183.5 %all-gather.3.cloned.1.call-start = ((), (), s32[]{:S(2)}) async-start(), calls=%async_computation.4 | async-start | bytes 3538944 | tf_op jit(solution)/shard_map/all_gather | solution.py:28
Sparse Core Ops, SparseCore 0:
  14.5 37.5 reduce-scatter.2
  54.3 34.7 reduce-scatter.4
  92.7 36.0 all-gather.2

commit v2 on v0

--- a/solution.py
+++ b/solution.py
@@ -2,6 +2,11 @@
 import jax.numpy as jnp
 from jax import lax
 from jax.sharding import PartitionSpec as P
+
+
+def axis_by_axis(array, inner_axis, outer_axis):
+    inner = lax.psum(array, inner_axis)
+    return lax.psum(inner, outer_axis)
 
 
 def task_squares(deltas):
@@ -17,7 +22,7 @@
     numerator = jnp.sum(weights * deltas.astype(jnp.float32), axis=0)
     denominator = jnp.sum(weights, axis=0)
     task_part = task_squares(deltas)
-    task_sq = lax.psum(task_part, ("task", "dp", "mp"))
+    task_sq = axis_by_axis(task_part, ("dp", "mp"), "task")
     numerator, denominator = (
         lax.psum_scatter(numerator, "task", scatter_dimension=0, tiled=True),
         lax.psum_scatter(denominator, "task", scatter_dimension=0, tiled=True),

time: 145 us -> 180 us (1.24)
  blocking collectives: 40.1 us -> 74.9 us
    psum x1 -> x3, blocking collectives: 40.1 us -> 74.9 us  [the longest x1 37 us: shards(): merged_sq = lax.psum(merged_part, ('task', 'dp', 'mp'))]
  transfers between devices with their start and end apart: 3 -> 3, of which waited for: 2 -> 2; matrix products, arithmetic and copies ran while one was open for 1% -> 0% of each run, Pallas kernels for 0% -> 0%
where the time goes in v2:
time: 180 us; the launch traced here: 179 us
  blocking collectives  74.9 us (42%)
  waiting for transfers between devices  74.7 us (42%)
  other arithmetic  15.1 us (8%)
  between operations  14.3 us (8%)
    reduce_scatter x1, waiting for transfers between devices, shards(): lax.psum_scatter(denominator, 'task', scatter_dimension=0, tiled=True)  37 us
    psum x1, blocking collectives, shards(): merged_sq = lax.psum(merged_part, ('task', 'dp', 'mp'))  37 us
    reduce_scatter x1, waiting for transfers between devices, shards(): lax.psum_scatter(numerator, 'task', scatter_dimension=0, tiled=True)  36.9 us
    psum x1, blocking collectives, axis_by_axis(): inner = lax.psum(array, inner_axis)  33 us
    reduce_sum x1, other arithmetic, task_squares(): own_sums = jnp.sum(widened * widened, axis=(1, 2))  7.85 us
    psum x1, blocking collectives, axis_by_axis(): return lax.psum(inner, outer_axis)  4.91 us
  transfers between devices with their start and end apart: 3, of which 2 were waited for; matrix products, arithmetic and copies ran while one was open for 0% of the time, Pallas kernels for 0%

profile of v2, /device:TPU:0, one launch (start us, length us, event | category | flops | bytes accessed | tf_op | source)
XLA Modules:
  0.0 179.3 jit_solution(15639292712771598451)
XLA Ops:
  6.5 0.0 reduce-scatter.3.cloned.1.call-start
  6.5 7.8 %fusion = (f32[3]{0:T(128)S(1)}, f32[256,2304]{1,0:T(8,128)}, f32[256,2304]{1,0:T(8,128)}) fusion(bf16[3,256,2304]{2,1,0:T(8,128)(2,1)} %param.2, bf16[3,256,2304]{2,1,0:T(8,128)(2,1)} %param.3), kind=kLoop, calls=%fused_computation.3 | loop fusion | flops 11206653 | bytes 11796492 | tf_op jit(solution)/shard_map/reduce_sum | solution.py:14
  14.4 0.0 reduce-scatter.3.cloned.1.call-update
  14.4 0.0 reduce-scatter.5.cloned.1.call-start
  14.5 0.7 reduce-scatter.5.cloned.1.call-update
  15.2 0.0 all-gather.2.cloned.1.call-start
  15.2 36.9 %reduce-scatter.3.cloned.1.call-done = f32[128,2304]{1,0:T(8,128)} async-done(((f32[256,2304]{1,0:T(8,128)}), f32[128,2304]{1,0:T(8,128)}) %reduce-scatter.3.cloned.1.call-update) | async-done | bytes 1179664 | tf_op jit(solution)/shard_map/reduce_scatter | solution.py:27
  52.1 37.0 %reduce-scatter.5.cloned.1.call-done = f32[128,2304]{1,0:T(8,128)} async-done(((f32[256,2304]{1,0:T(8,128)}), f32[128,2304]{1,0:T(8,128)}) %reduce-scatter.5.cloned.1.call-update) | async-done | bytes 1179664 | tf_op jit(solution)/shard_map/reduce_scatter | solution.py:28
  89.1 3.4 %multiply_reduce_fusion = (f32[]{:T(128)}, f32[128,2304]{1,0:T(8,128)}) fusion(f32[128,2304]{1,0:T(8,128)} %reduce-scatter.3.cloned.1.call-done, f32[128,2304]{1,0:T(8,128)} %reduce-scatter.5.cloned.1.call-done), kind=kLoop, calls=%fused_computation.6 | loop fusion | flops 884735 | bytes 3538948 | tf_op jit(solution)/shard_map/reduce_sum | solution.py:31
  92.6 0.0 all-gather.2.cloned.1.call-update
  92.6 0.2 dynamic_update_slice.3
  92.9 33.0 %psum.21 = f32[6]{0:T(128)S(1)} all-reduce(f32[6]{0:T(128)S(1)} %dynamic_update_slice.3), channel_id=1, replica_groups=mesh['task'=2,'dp'=8,'mp'=2] {'dp','mp'}, use_global_device_ids=true, to_apply=%region_1.0 | all-reduce | flops 6 | bytes 48 | tf_op jit(solution)/shard_map/psum | solution.py:8
  125.8 4.9 %psum.22 = f32[6]{0:T(128)S(1)} all-reduce(f32[6]{0:T(128)S(1)} %psum.21), channel_id=1, replica_groups=mesh['task'=2,'dp'=8,'mp'=2] {'task'}, use_global_device_ids=true, to_apply=%region_2.0 | all-reduce | flops 6 | bytes 48 | tf_op jit(solution)/shard_map/psum | solution.py:9
  130.8 0.6 sqrt_reduce_fusion
  131.9 37.0 %psum.23 = f32[]{:T(128)} all-reduce(f32[]{:T(128)} %get-tuple-element.8), channel_id=1, replica_groups=mesh['task'=2,'dp'=8,'mp'=2] {'task','dp','mp'}, use_global_device_ids=true, to_apply=%region_9.0 | all-reduce | flops 1 | bytes 8 | tf_op jit(solution)/shard_map/psum | solution.py:33
  169.5 0.0 all-gather.2.cloned.1.call-done
  169.6 3.2 %broadcast_multiply_fusion = f32[256,2304]{1,0:T(8,128)} fusion(f32[256,2304]{1,0:T(8,128)} %all-gather.2.cloned.1.call-done, f32[]{:T(128)S(6)} %div.11), kind=kLoop, calls=%fused_computation.5 | loop fusion | flops 589824 | bytes 4718596 | tf_op jit(solution)/shard_map/mul | solution.py:36
  (1 shorter events, 0.0 us)
Async XLA Ops:
  6.5 45.6 %reduce-scatter.3.cloned.1.call-start = ((), (), s32[]{:S(2)}) async-start(), calls=%async_computation.2 | async-start | bytes 3538944 | tf_op jit(solution)/shard_map/reduce_scatter | solution.py:27
  14.4 74.7 %reduce-scatter.5.cloned.1.call-start = ((), (), s32[]{:S(2)}) async-start(), calls=%async_computation.3 | async-start | bytes 3538944 | tf_op jit(solution)/shard_map/reduce_scatter | solution.py:28
  15.2 154.4 %all-gather.2.cloned.1.call-start = ((), (), s32[]{:S(2)}) async-start(), calls=%async_computation.4 | async-start | bytes 3538944 | tf_op jit(solution)/shard_map/all_gather | solution.py:32
Sparse Core Ops, SparseCore 0:
  14.5 37.5 reduce-scatter.2
  54.3 34.7 reduce-scatter.4
  92.7 36.0 all-gather.1
